TPU v7x, 32 devices: a whole 2x2x4 slice. The times are simulated.
32 devices in a mesh: dp: 16 (over z, y, x), tensor: 2 (over core).
Axes of the slice: x: 2, y: 2, z: 4, core: 2. Of those that a mesh axis runs over, the one named last changes fastest.
Arguments:
- encoded: bfloat16 [8192, 1152], P('dp', 'tensor'), may hold values from -9 to 9
- counts: int32 [128], P('dp'), may hold values from 16 to 64
- win_ids: int32 [128, 64], P('dp'), may hold values from 0 to 31, never falling along the last dimension, each value on 1 to 8 neighbouring positions
- dest_seq: int32 [128], P('dp'), may hold values from 0 to 15, as said below
- dest_slot: int32 [128], P('dp'), may hold values from 0 to 7, as said below
- w_first: bfloat16 [1152, 4608], P(None, 'tensor'), may hold values from -0.3125 to 0.3125
- b_first: float32 [4608], P('tensor'), may hold values from -3 to 3
- w_second: bfloat16 [4608, 2304], P('tensor'), may hold values from -0.1875 to 0.1875
- b_second: float32 [2304], P('tensor'), may hold values from -3 to 3
Outputs:
- projected: bfloat16 [4096, 2304], P('dp', 'tensor')
Inputs may be any that keep to these rules, and one draw needn't show every extreme that they name: `dest_seq`: every sequence receives exactly 8 samples, no two of them from the same index of dp. `dest_slot`: the samples that one sequence receives have distinct block offsets.
All inputs are finite; a program needn't handle non-finite values.
Results may differ from a plain program's by a relative error of at most 0.009.
Values may be sent and summed in bfloat16 or wider, within the bound.
A program may use at most 128 MiB of HBM per device.

v0:
```python
import jax
import jax.numpy as jnp
from jax import lax
from jax.sharding import PartitionSpec as P

BLOCK = 32


def pool_blocks(ids_live, tokens):
    windows = jnp.arange(BLOCK, dtype=jnp.int32)
    onehot = ids_live[:, None, :] == windows[None, :, None]
    number = jnp.sum(onehot.astype(jnp.float32), axis=2)
    totals = jnp.einsum(
        "nwc,ncf->nwf", onehot.astype(jnp.bfloat16), tokens, preferred_element_type=jnp.float32
    )
    return (totals / jnp.maximum(number, 1.0)[:, :, None]).astype(jnp.bfloat16)


def shards(encoded, counts, win_ids, dest_seq, dest_slot, w_first, b_first, w_second, b_second):
    samples = counts.shape[0]
    capacity = win_ids.shape[1]
    tokens = encoded.reshape(samples, capacity, encoded.shape[1])
    positions = jnp.arange(capacity, dtype=jnp.int32)
    ids_live = jnp.where(positions[None, :] < counts[:, None], win_ids, -1)
    groups = lax.axis_size("dp")
    targets = jnp.arange(groups, dtype=jnp.int32)
    chosen = dest_seq[None, :] == targets[:, None]
    picker = chosen.astype(jnp.bfloat16)
    offset_plus = jnp.sum(jnp.where(chosen, dest_slot[None, :] + 1, 0), axis=1)[:, None]
    pooled = pool_blocks(ids_live, tokens)
    outgoing = jnp.einsum("es,swf->ewf", picker, pooled, preferred_element_type=jnp.float32).astype(
        jnp.bfloat16
    )
    arrived, got_offset = (
        lax.all_to_all(outgoing, "dp", split_axis=0, concat_axis=0, tiled=True),
        lax.all_to_all(
            offset_plus.astype(jnp.bfloat16), "dp", split_axis=0, concat_axis=0, tiled=True
        ),
    )
    got_offset = got_offset.astype(jnp.int32)
    slot_from = got_offset[:, 0] - 1
    slot_ids = jnp.arange(samples, dtype=jnp.int32)
    placer = (slot_from[None, :] == slot_ids[:, None]).astype(jnp.bfloat16)
    packed = jnp.einsum("kd,dwf->kwf", placer, arrived, preferred_element_type=jnp.float32).astype(
        jnp.bfloat16
    )
    packed = packed.reshape(samples * arrived.shape[1], arrived.shape[2])
    preact = (
        jnp.dot(
            lax.all_gather(packed, "tensor", axis=1, tiled=True),
            w_first,
            preferred_element_type=jnp.float32,
        )
        + b_first
    )
    hidden = jax.nn.gelu(preact, approximate=True).astype(jnp.bfloat16)
    partial_value = jnp.dot(hidden, w_second, preferred_element_type=jnp.float32)
    summed = lax.psum_scatter(
        partial_value.astype(jnp.bfloat16), "tensor", scatter_dimension=1, tiled=True
    ).astype(jnp.float32)
    return (summed + b_second).astype(jnp.bfloat16)


def solution(mesh):
    placed = (
        P("dp", "tensor"),
        P("dp"),
        P("dp", None),
        P("dp"),
        P("dp"),
        P(None, "tensor"),
        P("tensor"),
        P("tensor", None),
        P("tensor"),
    )
    return jax.shard_map(
        shards, mesh=mesh, in_specs=placed, out_specs=P("dp", "tensor"), check_vma=False
    )
```

profile of v0, /device:TPU:1, one launch (start us, length us, event | category | flops | bytes accessed | tf_op | source)
XLA Modules:
  0.0 76.1 jit_solution(11469393669298495190)
XLA Ops:
  6.5 0.0 copy-start.1
  6.5 0.7 broadcast_add_fusion
  7.2 0.7 select_reduce_fusion
  8.0 0.7 copy.19
  8.7 7.4 %all-to-all-start = ((bf16[16,1,1]{2,1,0:T(2,128)(2,1)}), bf16[16,1,1]{2,1,0:T(2,128)(2,1)S(1)}, u32[]{:S(2)}, u32[]{:S(2)}) async-start(bf16[16,1,1]{2,1,0:T(2,128)(2,1)} %copy.19), calls=%async_computation | async-start | bytes 16384 | tf_op jit(solution)/shard_map/all_to_all | solution.py:36
  16.1 0.8 %fusion.16 = s32[8,64]{1,0:T(8,128)S(1)} fusion(s32[8,64]{1,0:T(8,128)} %param.11, s32[8]{0:T(128)} %param.10), kind=kLoop, calls=%fused_computation.28 | loop fusion | flops 1024 | bytes 4128 | tf_op jit(solution)/shard_map/jit(_where)/select_n | solution.py:24
  16.8 0.1 convert_reduce_fusion
  17.0 1.4 %copy.20 = bf16[512,576]{1,0:T(8,128)(2,1)S(1)} copy(bf16[512,576]{0,1:T(8,128)(2,1)} %param.9) | data formatting | bytes 1179648 | tf_op args[0]
  18.3 0.2 fusion.8
  18.6 0.0 copy-done.1
  18.6 0.4 convolution_convert_fusion.1
  19.0 1.0 %copy.22 = bf16[16,32,576]{2,1,0:T(8,128)(2,1)} copy(bf16[16,32,576]{2,0,1:T(8,128)(2,1)S(1)} %convolution_convert_fusion.1) | data formatting | bytes 1179648 | tf_op jit(solution)/shard_map/convert_element_type | solution.py:31
  20.0 0.0 copy-start.2
  20.0 2.1 %all-to-all-done = bf16[16,1,1]{2,1,0:T(2,128)(2,1)S(1)} async-done(((bf16[16,1,1]{2,1,0:T(2,128)(2,1)}), bf16[16,1,1]{2,1,0:T(2,128)(2,1)S(1)}, u32[]{:S(2)}, u32[]{:S(2)}) %all-to-all-start) | async-done | bytes 64 | tf_op jit(solution)/shard_map/all_to_all | solution.py:36
  22.1 4.3 %all-to-all-start.1 = ((bf16[16,32,576]{2,1,0:T(8,128)(2,1)}), bf16[16,32,576]{2,1,0:T(8,128)(2,1)S(1)}, u32[]{:S(2)}, u32[]{:S(2)}) async-start(bf16[16,32,576]{2,1,0:T(8,128)(2,1)} %copy.22), calls=%async_computation.1 | async-start | bytes 1310720 | tf_op jit(solution)/shard_map/all_to_all | solution.py:35
  26.5 0.0 reduce-scatter.4.cloned.1.call-start
  26.5 0.4 add_reduce_fusion
  26.9 13.5 %all-to-all-done.1 = bf16[16,32,576]{2,1,0:T(8,128)(2,1)S(1)} async-done(((bf16[16,32,576]{2,1,0:T(8,128)(2,1)}), bf16[16,32,576]{2,1,0:T(8,128)(2,1)S(1)}, u32[]{:S(2)}, u32[]{:S(2)}) %all-to-all-start.1) | async-done | bytes 589856 | tf_op jit(solution)/shard_map/all_to_all | solution.py:35
  40.4 0.3 convolution_convert_fusion.2
  40.7 0.2 copy.25
  40.9 6.3 %all_gather.3 = bf16[256,1152]{0,1:T(8,128)(2,1)S(1)} all-gather(bf16[256,576]{0,1:T(8,128)(2,1)S(1)} %copy.25), channel_id=1, replica_groups=mesh['dp'=16,'tensor'=2] {'tensor'}, dimensions={1}, use_global_device_ids=true | all-gather | bytes 884736 | tf_op jit(solution)/shard_map/all_gather | solution.py:50
  47.2 0.0 copy-done.2
  47.2 10.6 %convolution_convert_fusion = bf16[256,2304]{1,0:T(8,128)(2,1)S(1)} fusion(bf16[2304,2304]{1,0:T(8,128)(2,1)} %param.16, bf16[256,1152]{0,1:T(8,128)(2,1)S(1)} %all_gather.3, bf16[1152,2304]{1,0:T(8,128)(2,1)} %param.14, f32[2304]{0:T(1024)S(1)} %copy-done.2), kind=kOutput, calls=%fused_computation.1 | convolution fusion | flops 4083351552 | bytes 17703936 | tf_op jit(solution)/shard_map/dot_general | solution.py:57
  57.8 0.0 copy-start
  57.8 1.4 %copy.26 = bf16[256,2304]{0,1:T(8,128)(2,1)} copy(bf16[256,2304]{1,0:T(8,128)(2,1)S(1)} %convolution_convert_fusion) | data formatting | bytes 2359296
  59.2 0.0 reduce-scatter.4.cloned.1.call-update
  59.2 7.7 %reduce-scatter.4.cloned.1.call-done = bf16[1152,256]{1,0:T(8,128)(2,1)} async-done(((bf16[2304,256]{1,0:T(8,128)(2,1)}), bf16[1152,256]{1,0:T(8,128)(2,1)}) %reduce-scatter.4.cloned.1.call-update) | async-done | bytes 589840
  67.0 1.4 %copy.27 = bf16[256,1152]{1,0:T(8,128)(2,1)S(1)} copy(bf16[256,1152]{0,1:T(8,128)(2,1)} %bitcast.19) | data formatting | bytes 1179648
  68.3 0.0 copy-done
  68.3 0.9 %add_convert_fusion = bf16[256,1152]{1,0:T(8,128)(2,1)} fusion(bf16[256,1152]{1,0:T(8,128)(2,1)S(1)} %copy.27, f32[1152]{0:T(1024)S(1)} %copy-done), kind=kLoop, calls=%fused_computation.15 | loop fusion | flops 884736 | bytes 1184256 | tf_op jit(solution)/shard_map/convert_element_type | solution.py:61
  (3 shorter events, 0.0 us)
Async XLA Ops:
  6.5 12.0 %copy-start.1 = (s32[8]{0:T(128)S(1)}, s32[8]{0:T(128)}, u32[]{:S(2)}) copy-start(s32[8]{0:T(128)} %param.12) | copy-start | bytes 100
  8.7 13.5 %all-to-all-start = ((bf16[16,1,1]{2,1,0:T(2,128)(2,1)}), bf16[16,1,1]{2,1,0:T(2,128)(2,1)S(1)}, u32[]{:S(2)}, u32[]{:S(2)}) async-start(bf16[16,1,1]{2,1,0:T(2,128)(2,1)} %copy.19), calls=%async_computation | async-start | bytes 16384 | tf_op jit(solution)/shard_map/all_to_all | solution.py:36
  20.0 27.2 %copy-start.2 = (f32[2304]{0:T(1024)S(1)}, f32[2304]{0:T(1024)}, u32[]{:S(2)}) copy-start(f32[2304]{0:T(1024)} %param.15) | copy-start | bytes 27652
  22.1 18.3 %all-to-all-start.1 = ((bf16[16,32,576]{2,1,0:T(8,128)(2,1)}), bf16[16,32,576]{2,1,0:T(8,128)(2,1)S(1)}, u32[]{:S(2)}, u32[]{:S(2)}) async-start(bf16[16,32,576]{2,1,0:T(8,128)(2,1)} %copy.22), calls=%async_computation.1 | async-start | bytes 1310720 | tf_op jit(solution)/shard_map/all_to_all | solution.py:35
  26.5 40.5 %reduce-scatter.4.cloned.1.call-start = ((), (), s32[]{:S(2)}) async-start(), calls=%async_computation.3 | async-start | bytes 1769472
  57.8 10.5 %copy-start = (f32[1152]{0:T(1024)S(1)}, f32[1152]{0:T(1024)}, u32[]{:S(2)}) copy-start(f32[1152]{0:T(1024)} %param.17) | copy-start | bytes 13828
Sparse Core Ops, SparseCore 0:
  59.4 7.5 reduce-scatter.3
where the time goes:
time: 76.7 us; the launch traced here: 76.1 us
  waiting for transfers between devices  23.4 us (31%)
  between operations  13.5 us (18%)
  starting transfers between devices  11.8 us (15%)
  matrix products  11.6 us (15%)
  blocking collectives  6.26 us (8%)
  local copies, waits for them, and re-layouts  6 us (8%)
  other arithmetic  3.59 us (5%)
    all_to_all x1, waiting for transfers between devices, shards(): lax.all_to_all(outgoing, 'dp', split_axis=0, concat_axis=0, tiled=True)  13.5 us
    dot_general x1, matrix products, shards(): jnp.dot(hidden, w_second, preferred_element_type=jnp.float32)  10.6 us
    unnamed x2, waiting for transfers between devices  7.73 us
    all_to_all x1, starting transfers between devices, shards(): lax.all_to_all(offset_plus.astype(jnp.bfloat16), 'dp', split_axis=0, conc...  7.4 us
    all_gather x1, blocking collectives, shards(): lax.all_gather(packed, 'tensor', axis=1, tiled=True)  6.26 us
    all_to_all x1, starting transfers between devices, shards(): lax.all_to_all(outgoing, 'dp', split_axis=0, concat_axis=0, tiled=True)  4.34 us
    unnamed x9, local copies, waits for them, and re-layouts  4.15 us
    all_to_all x1, waiting for transfers between devices, shards(): lax.all_to_all(offset_plus.astype(jnp.bfloat16), 'dp', split_axis=0, conc...  2.15 us
  transfers between devices with their start and end apart: 3, of which 3 were waited for; matrix products, arithmetic and copies ran while one was open for 6% of the time, Pallas kernels for 0%

commit v1 on v0

v1 whole, which is shorter than its diff:
```python
import functools
import math

import jax
import jax.numpy as jnp
from jax import lax
from jax.experimental import pallas as pl
from jax.experimental.pallas import tpu as pltpu
from jax.sharding import PartitionSpec as P

BLOCK = 32
LANES = 128
MESH = pl.DeviceIdType.MESH
UNROLL_MAX = 16


def loop(count, body):
    if count <= UNROLL_MAX:
        for i in range(count):
            body(i)
    else:

        @pl.loop(0, count)
        def _(i):
            body(i)


def col_chunks(width, step):
    return [(lo, min(step, width - lo)) for lo in range(0, width, step)]


def gelu(x):
    c0 = math.sqrt(2.0 / math.pi)
    half = 0.5 * x
    return half + half * jnp.tanh(x * (c0 + (c0 * 0.044715) * (x * x)))


def kernel(
    dims,
    seq_s, slot_s, cnt_s, win_v, b1_v, b2_v, enc_h, w1_h, w2_h,
    out_v,
    enc, w1, w2, outgo, arr, sib, route_src, routes, xbuf, hidden, part_out, part_in,
    load_sem, w1_sem, w2_sem, send_sem, recv_sem, rsend_sem, rrecv_sem, fsend_sem, frecv_sem,
    psend_sem, precv_sem,
):
    groups, samples, cap, feat = dims
    full = feat // LANES
    rem = feat - full * LANES
    me = lax.axis_index("dp")
    core = lax.axis_index("tensor")
    other = 1 - core

    barrier = pltpu.get_barrier_semaphore()
    pl.semaphore_signal(barrier, 1, device_id={"tensor": other}, device_id_type=MESH)

    def greet(i):
        peer = lax.rem(me + 1 + i, groups)
        pl.semaphore_signal(barrier, 1, device_id={"dp": peer}, device_id_type=MESH)

    loop(groups - 1, greet)

    pairs = enc.shape[0]
    enc_copies = [
        pltpu.make_async_copy(enc_h.at[:, p * LANES : (p + 1) * LANES], enc.at[p], load_sem.at[p])
        for p in range(pairs)
    ]
    for copy in enc_copies:
        copy.start()

    wide = full * LANES
    mine = pl.multiple_of(core * feat, 64)
    theirs = pl.multiple_of(other * feat, 64)
    spans = [(mine, 0, wide), (theirs, wide, wide)]
    if rem:
        spans += [
            (pl.multiple_of(core * feat + wide, 64), 2 * wide, rem),
            (pl.multiple_of(other * feat + wide, 64), 2 * wide + rem, rem),
        ]
    w1_copies = [
        pltpu.make_async_copy(w1_h.at[pl.ds(src, size)], w1.at[pl.ds(dst, size)], w1_sem.at[n])
        for n, (src, dst, size) in enumerate(spans)
    ]
    half_out = w2.shape[2]
    w2_copies = [
        pltpu.make_async_copy(
            w2_h.at[:, pl.ds(pl.multiple_of(side * half_out, LANES), half_out)], w2.at[n], w2_sem.at[n]
        )
        for n, side in enumerate((other, core))
    ]
    for copy in w1_copies + w2_copies:
        copy.start()

    lane = lax.broadcasted_iota(jnp.int32, route_src.shape, 1)
    route = jnp.full(route_src.shape, -1, jnp.int32)
    for s in range(samples):
        route = jnp.where(lane == s, seq_s[s] * samples + slot_s[s], route)
    route_src[...] = route
    routes[0] = route

    per = LANES // cap
    windows = lax.broadcasted_iota(jnp.int32, (BLOCK, LANES), 0)
    lanes_at = lax.broadcasted_iota(jnp.int32, (BLOCK, LANES), 1)

    def pool(peer, dst):
        chosen = jnp.int32(0)
        for s in range(1, samples):
            chosen = jnp.where(seq_s[s] == peer, jnp.int32(s), chosen)
        pair = chosen // per
        start = (chosen - pair * per) * cap
        ids = jnp.concatenate([win_v[pl.ds(chosen, 1), :]] * per, axis=1)
        live = (lanes_at >= start) & (lanes_at < start + jnp.minimum(cnt_s[chosen], cap))
        hot = (ids == windows) & live
        hot_f = jnp.where(hot, 1.0, 0.0)
        number = jnp.sum(hot_f, axis=1, keepdims=True)
        total = lax.dot_general(
            hot_f.astype(jnp.bfloat16), enc[pair], (((1,), (1,)), ((), ())),
            preferred_element_type=jnp.float32,
        )
        y = (total * (1.0 / jnp.maximum(number, 1.0))).astype(jnp.bfloat16)
        for c in range(full):
            dst[c * BLOCK : (c + 1) * BLOCK, :] = y[:, c * LANES : (c + 1) * LANES]
        if rem:
            tail = y[:, wide:]
            mid = BLOCK // 2
            dst[full * BLOCK :, :] = jnp.concatenate([tail[:mid], tail[mid:]], axis=1)

    def far_first(i):
        off = (i + 1) // 2
        return groups // 2 + off * (2 * (i % 2) - 1)

    def data_copy(j):
        return pltpu.make_async_remote_copy(
            src_ref=outgo.at[j], dst_ref=arr.at[j], send_sem=send_sem.at[j], recv_sem=recv_sem.at[j],
            device_id={"dp": lax.rem(me + j, groups)}, device_id_type=MESH,
        )

    def route_copy(j):
        return pltpu.make_async_remote_copy(
            src_ref=route_src, dst_ref=routes.at[j], send_sem=rsend_sem.at[j], recv_sem=rrecv_sem.at[j],
            device_id={"dp": lax.rem(me + j, groups)}, device_id_type=MESH,
        )

    def forward(j):
        return pltpu.make_async_remote_copy(
            src_ref=arr.at[j], dst_ref=sib.at[j], send_sem=fsend_sem.at[j], recv_sem=frecv_sem.at[j],
            device_id={"tensor": other}, device_id_type=MESH,
        )

    for copy in enc_copies:
        copy.wait()
    first = far_first(0)
    pool(lax.rem(me + first, groups), outgo.at[first])
    pl.semaphore_wait(barrier, groups)

    def stage(i):
        j_next = far_first(i + 1)
        pool(lax.rem(me + j_next, groups), outgo.at[j_next])
        data_copy(far_first(i)).start()

    loop(groups - 2, stage)
    pool(me, arr.at[0])
    data_copy(far_first(groups - 2)).start()
    loop(groups - 1, lambda i: route_copy(i + 1).start())
    forward(0).start()

    def arrive(i):
        j = far_first(groups - 2 - i)
        data_copy(j).wait_recv()
        forward(j).start()

    loop(groups - 1, arrive)
    loop(groups - 1, lambda i: route_copy(i + 1).wait_recv())

    table = routes[...]
    source = lax.broadcasted_iota(jnp.int32, table.shape, 0)
    picks = [
        jnp.minimum(jnp.sum(jnp.where(table == me * samples + k, source, 0)), groups - 1)
        for k in range(samples)
    ]
    loop(groups, lambda i: forward(i).wait_recv())

    for k in range(samples):
        rows = slice(k * BLOCK, (k + 1) * BLOCK)
        for c in range(full):
            lanes = slice(c * LANES, (c + 1) * LANES)
            xbuf[rows, lanes] = arr[picks[k], c * BLOCK : (c + 1) * BLOCK, :]
            lanes = slice(wide + c * LANES, wide + (c + 1) * LANES)
            xbuf[rows, lanes] = sib[picks[k], c * BLOCK : (c + 1) * BLOCK, :]
        if rem:
            a = arr[picks[k], full * BLOCK :, :]
            b = sib[picks[k], full * BLOCK :, :]
            mid = BLOCK // 2
            lo = k * BLOCK
            xbuf[lo : lo + mid, 2 * wide :] = jnp.concatenate([a[:, :rem], b[:, :rem]], axis=1)
            xbuf[lo + mid : lo + 2 * mid, 2 * wide :] = jnp.concatenate([a[:, rem:], b[:, rem:]], axis=1)

    for copy in w1_copies:
        copy.wait()
    total_rows = samples * BLOCK
    step = min(256, total_rows)

    def first_layer(m):
        rows = pl.ds(m * step, step) if isinstance(m, int) else pl.ds(pl.multiple_of(m * step, step), step)
        for lo, size in col_chunks(w1.shape[1], 256):
            acc = jnp.dot(xbuf[rows, :], w1[:, lo : lo + size], preferred_element_type=jnp.float32)
            hidden[rows, lo : lo + size] = gelu(acc + b1_v[lo : lo + size]).astype(jnp.bfloat16)

    tiles = total_rows // step
    if tiles == 1:
        first_layer(0)
    else:
        pl.loop(0, tiles)(first_layer)
    for copy in w2_copies:
        copy.wait()

    chunks = col_chunks(half_out, 256)

    def part_copy(n):
        lo, size = chunks[n]
        return pltpu.make_async_remote_copy(
            src_ref=part_out.at[:, lo : lo + size], dst_ref=part_in.at[:, lo : lo + size],
            send_sem=psend_sem.at[n], recv_sem=precv_sem.at[n],
            device_id={"tensor": other}, device_id_type=MESH,
        )

    def over_rows(body):
        if tiles == 1:
            body(slice(0, step))
        else:

            @pl.loop(0, tiles)
            def _(m):
                body(pl.ds(pl.multiple_of(m * step, step), step))

    for n, (lo, size) in enumerate(chunks):

        def send_part(rows):
            part_out[rows, lo : lo + size] = jnp.dot(
                hidden[rows, :], w2[0, :, lo : lo + size], preferred_element_type=jnp.float32
            ).astype(jnp.bfloat16)

        over_rows(send_part)
        if n:
            part_copy(n - 1).start()
    for n, (lo, size) in enumerate(chunks):

        def keep_part(rows):
            out_v[rows, lo : lo + size] = jnp.dot(
                hidden[rows, :], w2[1, :, lo : lo + size], preferred_element_type=jnp.float32
            ).astype(jnp.bfloat16)

        over_rows(keep_part)
        if n == 0:
            part_copy(len(chunks) - 1).start()
    for n, (lo, size) in enumerate(chunks):
        part_copy(n).wait_recv()

        def finish(rows):
            lanes = slice(lo, lo + size)
            both = out_v[rows, lanes].astype(jnp.float32) + part_in[rows, lanes].astype(jnp.float32)
            out_v[rows, lanes] = (both + b2_v[lanes]).astype(jnp.bfloat16)

        over_rows(finish)
    loop(groups, lambda i: forward(i).wait_send())

    def drain(i):
        data_copy(i + 1).wait_send()
        route_copy(i + 1).wait_send()

    loop(groups - 1, drain)
    for n in range(len(chunks)):
        part_copy(n).wait_send()


def shards(encoded, counts, win_ids, dest_seq, dest_slot, w_first, b_first, w_second, b_second):
    samples, cap = win_ids.shape
    feat = encoded.shape[1]
    groups = lax.axis_size("dp")
    hid = w_first.shape[1]
    half_out = b_second.shape[0]
    rows = samples * BLOCK
    block_rows = BLOCK * feat // LANES
    chunks = len(col_chunks(half_out, 256))
    vmem = pl.BlockSpec(memory_space=pltpu.VMEM)
    smem = pl.BlockSpec(memory_space=pltpu.SMEM)
    hbm = pl.BlockSpec(memory_space=pltpu.HBM)
    bf16 = jnp.bfloat16
    dma = pltpu.SemaphoreType.DMA
    return pl.pallas_call(
        functools.partial(kernel, (groups, samples, cap, feat)),
        out_shape=jax.ShapeDtypeStruct((rows, half_out), bf16),
        in_specs=[smem, smem, smem, vmem, vmem, vmem, hbm, hbm, hbm],
        out_specs=vmem,
        scratch_shapes=[
            pltpu.VMEM((samples * cap // LANES, feat, LANES), bf16),
            pltpu.VMEM((2 * feat, hid), bf16),
            pltpu.VMEM((2, hid, half_out), bf16),
            pltpu.VMEM((groups, block_rows, LANES), bf16),
            pltpu.VMEM((groups, block_rows, LANES), bf16),
            pltpu.VMEM((groups, block_rows, LANES), bf16),
            pltpu.VMEM((1, LANES), jnp.int32),
            pltpu.VMEM((groups, 1, LANES), jnp.int32),
            pltpu.VMEM((rows, 2 * feat), bf16),
            pltpu.VMEM((rows, hid), bf16),
            pltpu.VMEM((rows, half_out), bf16),
            pltpu.VMEM((rows, half_out), bf16),
            dma((samples * cap // LANES,)), dma((4,)), dma((2,)),
            dma((groups,)), dma((groups,)), dma((groups,)), dma((groups,)), dma((groups,)), dma((groups,)),
            dma((chunks,)), dma((chunks,)),
        ],
        compiler_params=pltpu.CompilerParams(
            collective_id=0, has_side_effects=True, vmem_limit_bytes=60 * 1024 * 1024
        ),
    )(
        dest_seq, dest_slot, counts, win_ids, b_first, b_second, encoded.T, w_first, w_second,
    )


def solution(mesh):
    placed = (
        P("dp", "tensor"), P("dp"), P("dp", None), P("dp"), P("dp"),
        P(None, "tensor"), P("tensor"), P("tensor", None), P("tensor"),
    )
    return jax.shard_map(
        shards, mesh=mesh, in_specs=placed, out_specs=P("dp", "tensor"), check_vma=False
    )
```

time: 76.7 us -> 37.3 us (0.49)
  Pallas kernels: 0 us -> 35.2 us
  waiting for transfers between devices: 23.4 us -> 0 us
  between operations: 13.5 us -> 0.01 us
  starting transfers between devices: 11.8 us -> 0 us
  matrix products: 11.6 us -> 0 us
  blocking collectives: 6.26 us -> 0 us
  local copies, waits for them, and re-layouts: 6 us -> 1.92 us
  other arithmetic: 3.59 us -> 0 us
    pallas_call x0 -> x1, Pallas kernels: none -> 35.2 us  [shards(): pl.pallas_call(functools.partial(kernel, (groups, samples, cap, feat)), o...]
    all_to_all x2 -> x0, waiting for transfers between devices: 15.6 us -> none  [the longest x1 13.5 us: shards(): lax.all_to_all(outgoing, 'dp', split_axis=0, concat_axis=0, tiled=True)]
    all_to_all x2 -> x0, starting transfers between devices: 11.7 us -> none  [the longest x1 7.4 us: shards(): lax.all_to_all(offset_plus.astype(jnp.bfloat16), 'dp', split_axis=0, conc...]
    dot_general x4 -> x0, matrix products: 11.6 us -> none  [the longest x1 10.6 us: shards(): jnp.dot(hidden, w_second, preferred_element_type=jnp.float32)]
    unnamed x2 -> x0, waiting for transfers between devices: 7.73 us -> none
    all_gather x1 -> x0, blocking collectives: 6.26 us -> none  [shards(): lax.all_gather(packed, 'tensor', axis=1, tiled=True)]
    unnamed x9 -> x1, local copies, waits for them, and re-layouts: 4.15 us -> 1.92 us
    convert_element_type x3 -> x0, local copies, waits for them, and re-layouts: 1.69 us -> none  [the longest x1 0.95 us: shards(): jnp.einsum('es,swf->ewf', picker, pooled, preferred_element_type=jnp.floa...]
  transfers between devices with their start and end apart: 3 -> 0, of which waited for: 3 -> 0; matrix products, arithmetic and copies ran while one was open for 6% -> 0% of each run, Pallas kernels for 0% -> 0%
where the time goes in v1:
time: 37.3 us; the launch traced here: 37.1 us
  Pallas kernels  35.2 us (94%)
  local copies, waits for them, and re-layouts  1.92 us (5%)
    pallas_call x1, Pallas kernels, shards(): pl.pallas_call(functools.partial(kernel, (groups, samples, cap, feat)), o...  35.2 us
    unnamed x1, local copies, waits for them, and re-layouts  1.92 us

profile of v1, /device:TPU:1, one launch (start us, length us, event | category | flops | bytes accessed | tf_op | source)
XLA Modules:
  0.0 37.1 jit_solution(879229736160478041)
XLA Ops:
  0.0 35.2 %shard_map.91 = bf16[256,1152]{1,0:T(8,128)(2,1)} custom-call(s32[8]{0:T(128)} %seq_s.1, s32[8]{0:T(128)} %slot_s.1, s32[8]{0:T(128)} %cnt_s.1, s32[8,64]{1,0:T(8,128)} %win_v.1, f32[2304]{0:T(1024)} %b1_v.1, f32[1152]{0:T(1024)} %b2_v.1, bf16[576,512]{1,0:T(8,128)(2,1)} %bitcast.1, bf16[1152,2304]{1,0:T(8,128)(2,1)} %w1_h.1, bf16[2304,2304]{1,0:T(8,128)(2,1)} %w2_h.1), custom_call_target="tpu_custom_call" | custom-call | tf_op jit(solution)/shard_map/pallas_call | solution.py:289
  35.2 1.9 %copy.11 = bf16[256,1152]{1,0:T(8,128)(2,1)} copy(bf16[256,1152]{1,0:T(8,128)(2,1)} %shard_map.91) | data formatting | bytes 1179648

commit v2 on v1

--- a/solution.py
+++ b/solution.py
@@ -39,7 +39,7 @@
     dims,
     seq_s, slot_s, cnt_s, win_v, b1_v, b2_v, enc_h, w1_h, w2_h,
     out_v,
-    enc, w1, w2, outgo, arr, sib, route_src, routes, xbuf, hidden, part_out, part_in,
+    enc, w1, w2, pooled, outgo, arr, sib, route_src, routes, xbuf, hidden, part_out, part_in,
     load_sem, w1_sem, w2_sem, send_sem, recv_sem, rsend_sem, rrecv_sem, fsend_sem, frecv_sem,
     psend_sem, precv_sem,
 ):
@@ -101,32 +101,51 @@
     windows = lax.broadcasted_iota(jnp.int32, (BLOCK, LANES), 0)
     lanes_at = lax.broadcasted_iota(jnp.int32, (BLOCK, LANES), 1)
 
-    def pool(peer, dst):
+    def pool(s):
+        pair, part = divmod(s, per)
+        start = part * cap
+        ids = jnp.concatenate([win_v[s : s + 1, :]] * per, axis=1)
+        live = (lanes_at >= start) & (lanes_at < start + jnp.minimum(cnt_s[s], cap))
+        hot = jnp.where((ids == windows) & live, 1.0, 0.0)
+        number = jnp.sum(hot, axis=1, keepdims=True)
+        total = lax.dot_general(
+            hot.astype(jnp.bfloat16), enc[pair], (((1,), (1,)), ((), ())),
+            preferred_element_type=jnp.float32,
+        )
+        y = (total * (1.0 / jnp.maximum(number, 1.0))).astype(jnp.bfloat16)
+        for c in range(full):
+            pooled[s, c * BLOCK : (c + 1) * BLOCK, :] = y[:, c * LANES : (c + 1) * LANES]
+        if rem:
+            tail = y[:, wide:]
+            mid = BLOCK // 2
+            pooled[s, full * BLOCK :, :] = jnp.concatenate([tail[:mid], tail[mid:]], axis=1)
+
+    def pick(peer):
         chosen = jnp.int32(0)
         for s in range(1, samples):
             chosen = jnp.where(seq_s[s] == peer, jnp.int32(s), chosen)
-        pair = chosen // per
-        start = (chosen - pair * per) * cap
-        ids = jnp.concatenate([win_v[pl.ds(chosen, 1), :]] * per, axis=1)
-        live = (lanes_at >= start) & (lanes_at < start + jnp.minimum(cnt_s[chosen], cap))
-        hot = (ids == windows) & live
-        hot_f = jnp.where(hot, 1.0, 0.0)
-        number = jnp.sum(hot_f, axis=1, keepdims=True)
-        total = lax.dot_general(
-            hot_f.astype(jnp.bfloat16), enc[pair], (((1,), (1,)), ((), ())),
-            preferred_element_type=jnp.float32,
-        )
-        y = (total * (1.0 / jnp.maximum(number, 1.0))).astype(jnp.bfloat16)
-        for c in range(full):
-            dst[c * BLOCK : (c + 1) * BLOCK, :] = y[:, c * LANES : (c + 1) * LANES]
-        if rem:
-            tail = y[:, wide:]
-            mid = BLOCK // 2
-            dst[full * BLOCK :, :] = jnp.concatenate([tail[:mid], tail[mid:]], axis=1)
+        return pooled[chosen]
+
+    half = groups // 2
+    mine_base = me // half * half
+    far_base = half - mine_base
 
     def far_first(i):
-        off = (i + 1) // 2
-        return groups // 2 + off * (2 * (i % 2) - 1)
+        far = lax.rem(me + i, half)
+        near = lax.rem(me + i + 1, half)
+        late = i // half
+        peer = (1 - late) * (far_base + far) + late * (mine_base + near)
+        return lax.rem(peer - me + groups, groups)
+
+    def far_source(i):
+        far = lax.rem(me - i + groups, half)
+        near = lax.rem(me - i - 1 + 2 * groups, half)
+        late = i // half
+        peer = (1 - late) * (far_base + far) + late * (mine_base + near)
+        return lax.rem(me - peer + groups, groups)
+
+    def fill(j):
+        outgo[j] = pick(lax.rem(me + j, groups))
 
     def data_copy(j):
         return pltpu.make_async_remote_copy(
@@ -146,29 +165,24 @@
             device_id={"tensor": other}, device_id_type=MESH,
         )
 
-    for copy in enc_copies:
-        copy.wait()
-    first = far_first(0)
-    pool(lax.rem(me + first, groups), outgo.at[first])
+    for s in range(samples):
+        if s % per == 0:
+            enc_copies[s // per].wait()
+        pool(s)
+    loop(2, lambda i: fill(far_first(i)))
     pl.semaphore_wait(barrier, groups)
+    loop(groups - 1, lambda i: route_copy(i + 1).start())
 
     def stage(i):
-        j_next = far_first(i + 1)
-        pool(lax.rem(me + j_next, groups), outgo.at[j_next])
+        fill(far_first(i + 2))
         data_copy(far_first(i)).start()
 
-    loop(groups - 2, stage)
-    pool(me, arr.at[0])
+    loop(groups - 3, stage)
+    arr[0] = pick(me)
+    data_copy(far_first(groups - 3)).start()
     data_copy(far_first(groups - 2)).start()
-    loop(groups - 1, lambda i: route_copy(i + 1).start())
     forward(0).start()
 
-    def arrive(i):
-        j = far_first(groups - 2 - i)
-        data_copy(j).wait_recv()
-        forward(j).start()
-
-    loop(groups - 1, arrive)
     loop(groups - 1, lambda i: route_copy(i + 1).wait_recv())
 
     table = routes[...]
@@ -177,6 +191,12 @@
         jnp.minimum(jnp.sum(jnp.where(table == me * samples + k, source, 0)), groups - 1)
         for k in range(samples)
     ]
+    def arrive(i):
+        j = far_source(i)
+        data_copy(j).wait_recv()
+        forward(j).start()
+
+    loop(groups - 1, arrive)
     loop(groups, lambda i: forward(i).wait_recv())
 
     for k in range(samples):
@@ -201,7 +221,7 @@
 
     def first_layer(m):
         rows = pl.ds(m * step, step) if isinstance(m, int) else pl.ds(pl.multiple_of(m * step, step), step)
-        for lo, size in col_chunks(w1.shape[1], 256):
+        for lo, size in col_chunks(w1.shape[1], 768):
             acc = jnp.dot(xbuf[rows, :], w1[:, lo : lo + size], preferred_element_type=jnp.float32)
             hidden[rows, lo : lo + size] = gelu(acc + b1_v[lo : lo + size]).astype(jnp.bfloat16)
 
@@ -213,7 +233,7 @@
     for copy in w2_copies:
         copy.wait()
 
-    chunks = col_chunks(half_out, 256)
+    chunks = col_chunks(half_out, 384)
 
     def part_copy(n):
         lo, size = chunks[n]
@@ -280,7 +300,7 @@
     half_out = b_second.shape[0]
     rows = samples * BLOCK
     block_rows = BLOCK * feat // LANES
-    chunks = len(col_chunks(half_out, 256))
+    chunks = len(col_chunks(half_out, 384))
     vmem = pl.BlockSpec(memory_space=pltpu.VMEM)
     smem = pl.BlockSpec(memory_space=pltpu.SMEM)
     hbm = pl.BlockSpec(memory_space=pltpu.HBM)
@@ -295,6 +315,7 @@
             pltpu.VMEM((samples * cap // LANES, feat, LANES), bf16),
             pltpu.VMEM((2 * feat, hid), bf16),
             pltpu.VMEM((2, hid, half_out), bf16),
+            pltpu.VMEM((samples, block_rows, LANES), bf16),
             pltpu.VMEM((groups, block_rows, LANES), bf16),
             pltpu.VMEM((groups, block_rows, LANES), bf16),
             pltpu.VMEM((groups, block_rows, LANES), bf16),

time: 37.3 us -> 36 us (0.965)
  Pallas kernels: 35.2 us -> 33.9 us
    pallas_call x1, Pallas kernels: 35.2 us -> 33.9 us  [shards(): pl.pallas_call(functools.partial(kernel, (groups, samples, cap, feat)), o...]
where the time goes in v2:
time: 36 us; the launch traced here: 35.9 us
  Pallas kernels  33.9 us (94%)
  local copies, waits for them, and re-layouts  1.92 us (5%)
    pallas_call x1, Pallas kernels, shards(): pl.pallas_call(functools.partial(kernel, (groups, samples, cap, feat)), o...  33.9 us
    unnamed x1, local copies, waits for them, and re-layouts  1.92 us

profile of v2, /device:TPU:1, one launch (start us, length us, event | category | flops | bytes accessed | tf_op | source)
XLA Modules:
  0.0 35.9 jit_solution(13958118269306976978)
XLA Ops:
  0.0 33.9 %shard_map.91 = bf16[256,1152]{1,0:T(8,128)(2,1)} custom-call(s32[8]{0:T(128)} %seq_s.1, s32[8]{0:T(128)} %slot_s.1, s32[8]{0:T(128)} %cnt_s.1, s32[8,64]{1,0:T(8,128)} %win_v.1, f32[2304]{0:T(1024)} %b1_v.1, f32[1152]{0:T(1024)} %b2_v.1, bf16[576,512]{1,0:T(8,128)(2,1)} %bitcast.1, bf16[1152,2304]{1,0:T(8,128)(2,1)} %w1_h.1, bf16[2304,2304]{1,0:T(8,128)(2,1)} %w2_h.1), custom_call_target="tpu_custom_call" | custom-call | tf_op jit(solution)/shard_map/pallas_call | solution.py:309
  33.9 1.9 %copy.11 = bf16[256,1152]{1,0:T(8,128)(2,1)} copy(bf16[256,1152]{1,0:T(8,128)(2,1)} %shard_map.91) | data formatting | bytes 1179648
